TPU v7x, 32 devices: a whole 2x2x4 slice. The times are simulated.
32 devices in a mesh: groups: 2 (over x), seq: 16 (over z, y, core).
Axes of the slice: x: 2, y: 2, z: 4, core: 2. Of those that a mesh axis runs over, the one named last changes fastest.
Arguments:
- queries: bfloat16 [4096, 1792], P(('groups', 'seq')), parts along dimension 0, may hold values from -100 to 100
- key_rows: bfloat16 [4096, 256], P(('groups', 'seq')), parts along dimension 0, may hold values from -100 to 100
- value_rows: bfloat16 [4096, 256], P(('groups', 'seq')), parts along dimension 0, may hold values from -6 to 6
- span_order: int32 [64], P('groups'), parts along dimension 0, may hold values from 0 to 31, each once
- kept_blocks: int32 [4, 1], P('groups'), parts along dimension 0, may hold values from 0 to 3, as said below
Outputs:
- attended: bfloat16 [4096, 1792], P(('groups', 'seq')), parts along dimension 0
- kept_cache: bfloat16 [1024, 512], P(('groups', 'seq')), parts along dimension 0
There are 2 independent parts, one for each index of `groups`. A program takes and returns all parts, laid end to end along the dimension named above; each array names one. Nothing has to cross between parts.
Inputs may be any that keep to these rules, and one draw needn't show every extreme that they name: `kept_blocks`: each row lists 1 different blocks.
All inputs are finite; a program needn't handle non-finite values.
Results may differ from a plain program's by a relative error of at most 0.0055.
Values may be sent and summed in bfloat16 or wider, within the bound.
A program may use at most 64 MiB of HBM per device.

v0:
```python
import math

import jax
import jax.numpy as jnp
from jax import lax
from jax.sharding import PartitionSpec as P

HEAD_DIM = 128
BLOCK = 512


def token_positions(span_order, span_len):
    within = jnp.arange(span_len, dtype=jnp.int32)
    return (span_order[:, None] * span_len + within[None, :]).reshape(-1)


def cache_sources(kept_blocks, row_ids):
    block_ids = row_ids // BLOCK
    match = (
        jnp.arange(kept_blocks.shape[1], dtype=jnp.int32)[None, None, :] == block_ids[None, :, None]
    )
    chosen = jnp.sum(jnp.where(match, kept_blocks[:, None, :], 0), axis=-1)
    return chosen * BLOCK + row_ids[None, :] % BLOCK


def local(queries, key_rows, value_rows, span_order, kept_blocks):
    seq_count = lax.axis_size("seq")
    my_index = lax.axis_index("seq")
    query_rows = queries.shape[0]
    kv_heads = key_rows.shape[1] // HEAD_DIM
    group_size = queries.shape[1] // key_rows.shape[1]
    scale = 1.0 / math.sqrt(HEAD_DIM)
    positions = token_positions(span_order, query_rows // 2)
    query_pos = lax.dynamic_slice_in_dim(positions, my_index * query_rows, query_rows)
    query_heads = queries.reshape(query_rows, kv_heads, group_size, HEAD_DIM)
    cache_local = kept_blocks.shape[1] * BLOCK // seq_count
    cache_src = cache_sources(
        kept_blocks, my_index * cache_local + jnp.arange(cache_local, dtype=jnp.int32)
    )

    def pick_rows(sources, key_part, value_part, part_pos):
        onehot = (sources[:, :, None] == part_pos[None, None, :]).astype(jnp.bfloat16)
        count = key_part.shape[0]
        out_rows = sources.shape[1]
        picked_keys = jnp.einsum(
            "hrk,khd->rhd",
            onehot,
            key_part.reshape(count, kv_heads, HEAD_DIM),
            preferred_element_type=jnp.float32,
        )
        picked_values = jnp.einsum(
            "hrk,khd->rhd",
            onehot,
            value_part.reshape(count, kv_heads, HEAD_DIM),
            preferred_element_type=jnp.float32,
        )
        return jnp.concatenate(
            [picked_keys.reshape(out_rows, -1), picked_values.reshape(out_rows, -1)], axis=1
        )

    def attend_block(state, block_keys, block_values, block_pos):
        running_max, totals, accum = (state[0], state[1], state[2])
        count = block_keys.shape[0]
        scores = (
            jnp.einsum(
                "qhgd,khd->hgqk",
                query_heads,
                block_keys.reshape(count, kv_heads, HEAD_DIM),
                preferred_element_type=jnp.float32,
            )
            * scale
        )
        visible = block_pos[None, None, None, :] <= query_pos[None, None, :, None]
        scores = jnp.where(visible, scores, -1e30)
        new_max = jnp.maximum(running_max, jnp.max(scores, axis=-1))
        weights = jnp.where(visible, jnp.exp(scores - new_max[..., None]), 0.0)
        factor = jnp.exp(running_max - new_max)
        totals = totals * factor + jnp.sum(weights, axis=-1)
        mixed = jnp.einsum(
            "hgqk,khd->hgqd",
            weights.astype(jnp.bfloat16),
            block_values.reshape(count, kv_heads, HEAD_DIM),
            preferred_element_type=jnp.float32,
        )
        accum = accum * factor[..., None] + mixed
        return (new_max, totals, accum)

    initial = (
        jnp.full((kv_heads, group_size, query_rows), -1e30, jnp.float32),
        jnp.zeros((kv_heads, group_size, query_rows), jnp.float32),
        jnp.zeros((kv_heads, group_size, query_rows, HEAD_DIM), jnp.float32),
    )
    initial = initial + (jnp.zeros((cache_local, 2 * kv_heads * HEAD_DIM), jnp.float32),)
    piece_keys = lax.all_gather(key_rows, "seq", axis=0, tiled=True)
    piece_values = lax.all_gather(value_rows, "seq", axis=0, tiled=True)
    count = piece_keys.shape[0]
    width = math.gcd(count, 512)

    def inner(step_index, inner_state):
        offset = (step_index * width).astype(jnp.int32)
        block_keys = lax.dynamic_slice_in_dim(piece_keys, offset, width, 0)
        block_values = lax.dynamic_slice_in_dim(piece_values, offset, width, 0)
        block_pos = lax.dynamic_slice_in_dim(positions, offset, width)
        updated = attend_block(inner_state, block_keys, block_values, block_pos)
        extra = (inner_state[3] + pick_rows(cache_src, block_keys, block_values, block_pos),)
        return updated + extra

    final = lax.fori_loop(0, count // width, inner, initial)
    attended = final[2] / final[1][..., None]
    attended = jnp.transpose(attended, (2, 0, 1, 3)).reshape(query_rows, -1).astype(jnp.bfloat16)
    kept_cache = final[3].astype(jnp.bfloat16)
    return (attended, kept_cache)


def solution(mesh):
    placed = (
        P(("groups", "seq"), None),
        P(("groups", "seq"), None),
        P(("groups", "seq"), None),
        P("groups"),
        P("groups", None),
    )
    return jax.shard_map(
        local,
        mesh=mesh,
        in_specs=placed,
        out_specs=(P(("groups", "seq"), None), P(("groups", "seq"), None)),
        check_vma=False,
    )
```

profile of v0, /device:TPU:0, one launch (start us, length us, event | category | flops | bytes accessed | tf_op | source)
XLA Modules:
  0.0 120.7 jit_solution(2158012903326060525)
XLA Ops:
  7.2 1.6 %copy.16 = bf16[128,256]{0,1:T(8,128)(2,1)} copy(bf16[128,256]{1,0:T(8,128)(2,1)} %param.8) | data formatting | bytes 131072 | tf_op args[1]
  8.9 1.6 %copy.18 = bf16[128,256]{0,1:T(8,128)(2,1)} copy(bf16[128,256]{1,0:T(8,128)(2,1)} %param.9) | data formatting | bytes 131072 | tf_op args[2]
  10.5 0.7 broadcast_multiply_fusion
  11.3 1.3 %copy.17 = bf16[128,1792]{0,1:T(8,128)(2,1)S(1)} copy(bf16[128,1792]{1,0:T(8,128)(2,1)} %param.7) | data formatting | bytes 917504 | tf_op args[0]
  12.6 0.3 copy.19
  12.9 0.1 dynamic_slice.24
  13.0 37.1 %all-gather.3.cloned.1.call-done = bf16[2048,256]{0,1:T(8,128)(2,1)} async-done(((bf16[128,256]{0,1:T(8,128)(2,1)}), bf16[2048,256]{0,1:T(8,128)(2,1)}) %all-gather.3.cloned.1.call-update) | async-done | bytes 1048592 | tf_op jit(solution)/shard_map/all_gather | solution.py:94
  50.1 38.4 %all-gather.5.cloned.1.call-done = bf16[2048,256]{0,1:T(8,128)(2,1)} async-done(((bf16[128,256]{0,1:T(8,128)(2,1)}), bf16[2048,256]{0,1:T(8,128)(2,1)}) %all-gather.5.cloned.1.call-update) | async-done | bytes 1048592 | tf_op jit(solution)/shard_map/all_gather | solution.py:95
  88.5 23.3 %while.20 = (s32[]{:T(128)}, f32[2,7,128]{2,1,0:T(8,128)S(1)}, f32[2,7,128]{2,1,0:T(8,128)S(1)}, f32[2,7,128,128]{3,2,1,0:T(8,128)S(1)}, f32[32,512]{1,0:T(8,128...) while((s32[]{:T(128)}, f32[2,7,128]{2,1,0:T(8,128)S(1)}, ...), condition=%wide.region_3.4_spmd.clone, body=%wide.region_0.3_spmd.clone.sunk | while | flops 499344320 | bytes 16182928 | solution.py:108
  88.5 0.7 multiply_add_fusion.2
  89.3 0.1 dynamic_slice.33
  89.3 0.1 broadcast_compare_fusion.2
  89.5 1.1 constant_dynamic-slice_fusion.3
  90.6 0.2 convolution_bitcast_fusion.4
  90.8 0.2 convolution_bitcast_fusion.5
  91.1 0.8 fusion.47
  91.9 0.9 fusion.48
  92.8 1.5 %fusion.50 = f32[2,7,128,128]{3,2,1,0:T(8,128)S(1)} fusion(bf16[512,2,128,1]{0,2,3,1:T(8,128)(2,1)S(1)} %bitcast.80, f32[2,512,128,7]{2,1,3,0:T(8,128)S(1)} %get-tuple-element.372, f32[2,7,128]{2,1,0:T(8,128)S(1)} %select_maximum_fusion.2, pred[128,512]{0,1:T(8,128)(4,1)S(1)} %broadcast_compare_fusion.2, ...), kind=kOutput, calls=%fused_computation.8.clone.1 | convolution fusion | flops 240156672 | bytes 5847041 | tf_op jit(solution)/shard_map/while/body/eval_jaxpr/hgqk,khd->hgqd/dot_general | solution.py:79
  94.4 0.7 multiply_add_fusion.2
  95.1 0.1 dynamic_slice.33
  95.2 0.1 broadcast_compare_fusion.2
  95.3 1.1 constant_dynamic-slice_fusion.3
  96.4 0.2 convolution_bitcast_fusion.4
  96.6 0.2 convolution_bitcast_fusion.5
  96.9 0.8 fusion.47
  97.7 0.9 fusion.48
  98.6 1.5 %fusion.50 = f32[2,7,128,128]{3,2,1,0:T(8,128)S(1)} fusion(bf16[512,2,128,1]{0,2,3,1:T(8,128)(2,1)S(1)} %bitcast.80, f32[2,512,128,7]{2,1,3,0:T(8,128)S(1)} %get-tuple-element.372, f32[2,7,128]{2,1,0:T(8,128)S(1)} %select_maximum_fusion.2, pred[128,512]{0,1:T(8,128)(4,1)S(1)} %broadcast_compare_fusion.2, ...), kind=kOutput, calls=%fused_computation.8.clone.1 | convolution fusion | flops 240156672 | bytes 5847041 | tf_op jit(solution)/shard_map/while/body/eval_jaxpr/hgqk,khd->hgqd/dot_general | solution.py:79
  100.2 0.7 multiply_add_fusion.2
  101.0 0.1 broadcast_compare_fusion.2
  101.1 1.1 constant_dynamic-slice_fusion.3
  102.2 0.2 convolution_bitcast_fusion.4
  102.4 0.2 convolution_bitcast_fusion.5
  102.7 0.8 fusion.47
  103.5 0.9 fusion.48
  104.4 1.5 %fusion.50 = f32[2,7,128,128]{3,2,1,0:T(8,128)S(1)} fusion(bf16[512,2,128,1]{0,2,3,1:T(8,128)(2,1)S(1)} %bitcast.80, f32[2,512,128,7]{2,1,3,0:T(8,128)S(1)} %get-tuple-element.372, f32[2,7,128]{2,1,0:T(8,128)S(1)} %select_maximum_fusion.2, pred[128,512]{0,1:T(8,128)(4,1)S(1)} %broadcast_compare_fusion.2, ...), kind=kOutput, calls=%fused_computation.8.clone.1 | convolution fusion | flops 240156672 | bytes 5847041 | tf_op jit(solution)/shard_map/while/body/eval_jaxpr/hgqk,khd->hgqd/dot_general | solution.py:79
  106.0 0.7 multiply_add_fusion.2
  106.7 0.1 dynamic_slice.33
  106.8 0.1 broadcast_compare_fusion.2
  106.9 1.1 constant_dynamic-slice_fusion.3
  108.0 0.2 convolution_bitcast_fusion.4
  108.3 0.2 convolution_bitcast_fusion.5
  108.5 0.8 fusion.47
  109.3 0.9 fusion.48
  110.2 1.5 %fusion.50 = f32[2,7,128,128]{3,2,1,0:T(8,128)S(1)} fusion(bf16[512,2,128,1]{0,2,3,1:T(8,128)(2,1)S(1)} %bitcast.80, f32[2,512,128,7]{2,1,3,0:T(8,128)S(1)} %get-tuple-element.372, f32[2,7,128]{2,1,0:T(8,128)S(1)} %select_maximum_fusion.2, pred[128,512]{0,1:T(8,128)(4,1)S(1)} %broadcast_compare_fusion.2, ...), kind=kOutput, calls=%fused_computation.8.clone.1 | convolution fusion | flops 240156672 | bytes 5847041 | tf_op jit(solution)/shard_map/while/body/eval_jaxpr/hgqk,khd->hgqd/dot_general | solution.py:79
  111.8 0.3 copy.20
  112.1 0.1 divide_convert_fusion
  112.2 1.0 copy.21
  113.2 0.6 convert_element_type.25
  (37 shorter events, 0.6 us)
Async XLA Ops:
  7.2 42.9 %all-gather.3.cloned.1.call-start = ((), (), s32[]{:S(2)}) async-start(), calls=%async_computation | async-start | bytes 1114112 | tf_op jit(solution)/shard_map/all_gather | solution.py:94
  8.8 79.7 %all-gather.5.cloned.1.call-start = ((), (), s32[]{:S(2)}) async-start(), calls=%async_computation.1 | async-start | bytes 1114112 | tf_op jit(solution)/shard_map/all_gather | solution.py:95
Sparse Core Ops, SparseCore 0:
  10.7 39.3 all-gather.2
  52.3 36.2 all-gather.4
where the time goes:
time: 121 us
  waiting for transfers between devices  75.6 us (62%)
  between operations  14.1 us (12%)
  matrix products  11 us (9%)
  local copies, waits for them, and re-layouts  10.8 us (9%)
  other arithmetic  8.65 us (7%)
    all_gather x1, waiting for transfers between devices, local(): piece_values = lax.all_gather(value_rows, 'seq', axis=0, tiled=True)  38.4 us
    all_gather x1, waiting for transfers between devices, local(): piece_keys = lax.all_gather(key_rows, 'seq', axis=0, tiled=True)  37.1 us
    dot_general x4, matrix products, attend_block(): jnp.einsum('hgqk,khd->hgqd', weights.astype(jnp.bfloat16), block_values.r...  6.16 us
    unnamed x5, local copies, waits for them, and re-layouts  5.68 us
    dynamic_slice x4, local copies, waits for them, and re-layouts, inner(): block_values = lax.dynamic_slice_in_dim(piece_values, offset, width, 0)  4.29 us
    reduce_sum x4, other arithmetic, attend_block(): totals = totals * factor + jnp.sum(weights, axis=-1)  3.54 us
    dot_general x4, matrix products, attend_block(): jnp.einsum('qhgd,khd->hgqk', query_heads, block_keys.reshape(count, kv_he...  3.13 us
    add x4, other arithmetic, cache_sources(): return chosen * BLOCK + row_ids[None, :] % BLOCK  2.91 us
  transfers between devices with their start and end apart: 2, of which 2 were waited for; matrix products, arithmetic and copies ran while one was open for 3% of the time, Pallas kernels for 0%

commit v1 on v0

--- a/solution.py
+++ b/solution.py
@@ -1,8 +1,11 @@
+import functools
 import math
 
 import jax
 import jax.numpy as jnp
 from jax import lax
+from jax.experimental import pallas as pl
+from jax.experimental.pallas import tpu as pltpu
 from jax.sharding import PartitionSpec as P
 
 HEAD_DIM = 128
@@ -23,7 +26,7 @@
     return chosen * BLOCK + row_ids[None, :] % BLOCK
 
 
-def local(queries, key_rows, value_rows, span_order, kept_blocks):
+def local_plain(queries, key_rows, value_rows, span_order, kept_blocks):
     seq_count = lax.axis_size("seq")
     my_index = lax.axis_index("seq")
     query_rows = queries.shape[0]
@@ -111,6 +114,231 @@
     kept_cache = final[3].astype(jnp.bfloat16)
     return (attended, kept_cache)
 
+VMEM_BUDGET = 44 * 1024 * 1024
+MASKED = -1e30
+
+
+def ring_place(chip, chips):
+    odd = chip % 2
+    return (1 - odd) * (chip // 2) + odd * (chips - 1 - chip // 2)
+
+
+def ring_chip(place, chips):
+    back = place // (chips // 2)
+    return (1 - back) * 2 * place + back * (2 * (chips - 1 - place) + 1)
+
+
+def fused_kernel(
+    chips,
+    span_ref,
+    kept_ref,
+    q_ref,
+    k_ref,
+    v_ref,
+    out_ref,
+    cache_ref,
+    k_all,
+    v_all,
+    scores,
+    weights,
+    row_max,
+    send_sem,
+    recv_sem,
+):
+    rows = k_ref.shape[0]
+    span_len = rows // 2
+    pair = 2 * rows
+    kv_heads = k_ref.shape[1] // HEAD_DIM
+    heads = q_ref.shape[1] // HEAD_DIM
+    group = heads // kv_heads
+    factor = math.log2(math.e) / math.sqrt(HEAD_DIM)
+
+    me = lax.axis_index("seq")
+    chip, core = me // 2, me % 2
+    place = ring_place(chip, chips)
+    partner = 2 * chip + 1 - core
+
+    def chip_at(step):
+        return ring_chip((place + step + 2 * chips) % chips, chips)
+
+    right = 2 * chip_at(1) + core
+    left = 2 * chip_at(-1) + core
+
+    barrier = pltpu.get_barrier_semaphore()
+    for other in (left, right, partner):
+        pl.semaphore_signal(
+            barrier, inc=1, device_id={"seq": other}, device_id_type=pl.DeviceIdType.MESH
+        )
+    pl.semaphore_wait(barrier, 3)
+
+    long_way = chips // 2
+    short_way = chips - 1 - long_way
+    reach = {("k", 1): long_way, ("k", -1): short_way, ("v", 1): short_way, ("v", -1): long_way}
+    own = {"k": k_ref, "v": v_ref}
+    gathered = {"k": k_all, "v": v_all}
+    counter = [0]
+
+    def tile(kind, index):
+        return gathered[kind].at[pl.ds(pl.multiple_of(index * rows, rows), rows), :]
+
+    def message(kind, step, target):
+        index = 2 * chip_at(step) + core
+        slot = counter[0]
+        counter[0] += 1
+        return pltpu.make_async_remote_copy(
+            src_ref=own[kind] if step == 0 else tile(kind, index),
+            dst_ref=tile(kind, index),
+            send_sem=send_sem.at[slot],
+            recv_sem=recv_sem.at[slot],
+            device_id={"seq": target},
+            device_id_type=pl.DeviceIdType.MESH,
+        )
+
+    hops, crossings = {}, {}
+    for kind in ("k", "v"):
+        for way in (1, -1):
+            for hop in range(1, reach[kind, way] + 1):
+                hops[kind, way, hop] = message(kind, -way * (hop - 1), right if way == 1 else left)
+        crossings[kind, 0] = message(kind, 0, partner)
+        for way in (1, -1):
+            for hop in range(1, reach[kind, way] + 1):
+                crossings[kind, -way * hop] = message(kind, -way * hop, partner)
+
+    for kind in ("k", "v"):
+        hops[kind, 1, 1].start()
+        hops[kind, -1, 1].start()
+        crossings[kind, 0].start()
+
+    def relay(kind, hop):
+        for way in (1, -1):
+            if hop <= reach[kind, way]:
+                hops[kind, way, hop].wait_recv()
+                if hop < reach[kind, way]:
+                    hops[kind, way, hop + 1].start()
+                crossings[kind, -way * hop].start()
+
+    own_rows = pl.ds(pl.multiple_of(me * rows, rows), rows)
+    k_all[own_rows, :] = k_ref[...]
+    v_all[own_rows, :] = v_ref[...]
+
+    row_ids = lax.broadcasted_iota(jnp.int32, (rows, pair), 0)
+    key_ids = lax.broadcasted_iota(jnp.int32, (rows, pair), 1)
+    query_pos = (
+        jnp.where(row_ids < span_len, span_ref[2 * me], span_ref[2 * me + 1]) * span_len
+        + row_ids % span_len
+    )
+
+    def score_chip(step):
+        at = chip_at(step)
+        s0, s1, s2, s3 = (span_ref[4 * at + i] for i in range(4))
+        spans = jnp.where(
+            key_ids < rows,
+            jnp.where(key_ids < span_len, s0, s1),
+            jnp.where(key_ids < rows + span_len, s2, s3),
+        )
+        key_pos = spans * span_len + key_ids % span_len
+        bias = jnp.where(key_pos <= query_pos, 0.0, MASKED)
+        key_rows = pl.ds(pl.multiple_of(at * pair, pair), pair)
+        for h in range(kv_heads):
+            keys = k_all[key_rows, h * HEAD_DIM : (h + 1) * HEAD_DIM]
+            for g in range(group):
+                j = h * group + g
+                s = lax.dot_general(
+                    q_ref[:, j * HEAD_DIM : (j + 1) * HEAD_DIM],
+                    keys,
+                    (((1,), (1,)), ((), ())),
+                    preferred_element_type=jnp.float32,
+                )
+                s = s * factor + bias
+                scores[j, :, key_rows] = s
+                top = jnp.maximum(s[:, :rows], s[:, rows:])
+                row_max[j] = top if step == 0 else jnp.maximum(row_max[j], top)
+
+    crossings["k", 0].wait_recv()
+    score_chip(0)
+    for hop in range(1, long_way + 1):
+        relay("k", hop)
+        relay("v", hop)
+        for way in (1, -1):
+            if hop <= reach["k", way]:
+                crossings["k", -way * hop].wait_recv()
+                score_chip(-way * hop)
+
+    for j in range(heads):
+        top = jnp.max(row_max[j], axis=1, keepdims=True)
+        weights[j] = jnp.exp2(scores[j] - top).astype(jnp.bfloat16)
+
+    for step in range(-(chips - 1), chips):
+        if ("v", step) in crossings:
+            crossings["v", step].wait_recv()
+
+    cache_rows = cache_ref.shape[0]
+    first = me * cache_rows
+    within = pl.multiple_of(first % span_len, cache_rows)
+    for h in range(kv_heads):
+        span = kept_ref[h, first // BLOCK] * (BLOCK // span_len) + first % BLOCK // span_len
+        columns = slice(h * HEAD_DIM, (h + 1) * HEAD_DIM)
+        later = slice((kv_heads + h) * HEAD_DIM, (kv_heads + h + 1) * HEAD_DIM)
+        picked_keys = jnp.zeros((cache_rows, HEAD_DIM), jnp.float32)
+        picked_values = jnp.zeros((cache_rows, HEAD_DIM), jnp.float32)
+        for s in range(span_ref.shape[0]):
+            chosen = jnp.where(span_ref[s] == span, 1.0, 0.0)
+            source = pl.ds(s * span_len + within, cache_rows)
+            picked_keys += k_all[source, columns].astype(jnp.float32) * chosen
+            picked_values += v_all[source, columns].astype(jnp.float32) * chosen
+        cache_ref[:, columns] = picked_keys.astype(cache_ref.dtype)
+        cache_ref[:, later] = picked_values.astype(cache_ref.dtype)
+
+    ones = jnp.ones((v_all.shape[0], HEAD_DIM), jnp.bfloat16)
+    for h in range(kv_heads):
+        values = jnp.concatenate([v_all[:, h * HEAD_DIM : (h + 1) * HEAD_DIM], ones], axis=1)
+        for g in range(group):
+            j = h * group + g
+            mixed = jnp.dot(weights[j], values, preferred_element_type=jnp.float32)
+            out_ref[:, j * HEAD_DIM : (j + 1) * HEAD_DIM] = (
+                mixed[:, :HEAD_DIM] / mixed[:, HEAD_DIM:]
+            ).astype(out_ref.dtype)
+
+    for copy in (*hops.values(), *crossings.values()):
+        copy.wait_send()
+
+
+def local(queries, key_rows, value_rows, span_order, kept_blocks):
+    seq_count = lax.axis_size("seq")
+    rows = key_rows.shape[0]
+    heads = queries.shape[1] // HEAD_DIM
+    tokens = rows * seq_count
+    cache_local = kept_blocks.shape[1] * BLOCK // seq_count
+    span_len = rows // 2
+    fits = heads * rows * tokens * 6 + 4 * tokens * key_rows.shape[1] <= VMEM_BUDGET
+    if not fits or seq_count < 8 or span_len % cache_local or cache_local % 16:
+        return local_plain(queries, key_rows, value_rows, span_order, kept_blocks)
+    chips = seq_count // 2
+    messages = 2 * (2 * chips - 1)
+    vmem = pl.BlockSpec(memory_space=pltpu.VMEM)
+    smem = pl.BlockSpec(memory_space=pltpu.SMEM)
+    return pl.pallas_call(
+        functools.partial(fused_kernel, chips),
+        out_shape=(
+            jax.ShapeDtypeStruct(queries.shape, jnp.bfloat16),
+            jax.ShapeDtypeStruct((cache_local, 2 * key_rows.shape[1]), jnp.bfloat16),
+        ),
+        in_specs=[smem, smem, vmem, vmem, vmem],
+        out_specs=(vmem, vmem),
+        scratch_shapes=[
+            pltpu.VMEM((tokens, key_rows.shape[1]), jnp.bfloat16),
+            pltpu.VMEM((tokens, key_rows.shape[1]), jnp.bfloat16),
+            pltpu.VMEM((heads, rows, tokens), jnp.float32),
+            pltpu.VMEM((heads, rows, tokens), jnp.bfloat16),
+            pltpu.VMEM((heads, rows, HEAD_DIM), jnp.float32),
+            pltpu.SemaphoreType.DMA((messages,)),
+            pltpu.SemaphoreType.DMA((messages,)),
+        ],
+        compiler_params=pltpu.CompilerParams(
+            collective_id=0, has_side_effects=True, vmem_limit_bytes=60 * 1024 * 1024
+        ),
+    )(span_order, kept_blocks, queries, key_rows, value_rows)
+
 
 def solution(mesh):
     placed = (

time: 121 us -> 31.8 us (0.26)
  waiting for transfers between devices: 75.6 us -> 0 us
  Pallas kernels: 0 us -> 27.3 us
  between operations: 14.1 us -> 0.65 us
  matrix products: 11 us -> 0 us
  other arithmetic: 8.65 us -> 0 us
  local copies, waits for them, and re-layouts: 10.8 us -> 3.74 us
    all_gather x2 -> x0, waiting for transfers between devices: 75.6 us -> none  [the longest x1 38.4 us: local(): piece_values = lax.all_gather(value_rows, 'seq', axis=0, tiled=True)]
    pallas_call x0 -> x1, Pallas kernels: none -> 27.3 us  [local(): pl.pallas_call(functools.partial(fused_kernel, chips), out_shape=(jax.Sha...]
    dot_general x16 -> x0, matrix products: 11 us -> none  [the longest x4 6.16 us: attend_block(): jnp.einsum('hgqk,khd->hgqd', weights.astype(jnp.bfloat16), block_values.r...]
    dynamic_slice x9 -> x0, local copies, waits for them, and re-layouts: 4.67 us -> none  [the longest x4 4.29 us: inner(): block_values = lax.dynamic_slice_in_dim(piece_values, offset, width, 0)]
    reduce_sum x4 -> x0, other arithmetic: 3.54 us -> none  [attend_block(): totals = totals * factor + jnp.sum(weights, axis=-1)]
    add x13 -> x0, other arithmetic: 3.12 us -> none  [the longest x4 2.91 us: cache_sources(): return chosen * BLOCK + row_ids[None, :] % BLOCK]
    unnamed x5, local copies, waits for them, and re-layouts: 5.68 us -> 3.74 us
  transfers between devices with their start and end apart: 2 -> 0, of which waited for: 2 -> 0; matrix products, arithmetic and copies ran while one was open for 3% -> 0% of each run, Pallas kernels for 0% -> 0%
where the time goes in v1:
time: 31.8 us; the launch traced here: 31.7 us
  Pallas kernels  27.3 us (86%)
  local copies, waits for them, and re-layouts  3.74 us (12%)
  between operations  0.65 us (2%)
    pallas_call x1, Pallas kernels, local(): pl.pallas_call(functools.partial(fused_kernel, chips), out_shape=(jax.Sha...  27.3 us
    unnamed x5, local copies, waits for them, and re-layouts  3.74 us

profile of v1, /device:TPU:0, one launch (start us, length us, event | category | flops | bytes accessed | tf_op | source)
XLA Modules:
  0.0 31.7 jit_solution(9227885125817892190)
XLA Ops:
  0.6 1.3 %copy.7.kept_ref = s32[2,1]{1,0:T(2,128)} copy(s32[2,1]{0,1:T(1,128)} %param.9) | data formatting | bytes 16 | tf_op args[4]
  1.9 27.3 %shard_map.68 = (bf16[128,1792]{1,0:T(8,128)(2,1)}, bf16[32,512]{1,0:T(8,128)(2,1)}) custom-call(s32[32]{0:T(128)} %span_ref.1, s32[2,1]{1,0:T(2,128)} %copy.7.kept_ref, bf16[128,1792]{1,0:T(8,128)(2,1)} %q_ref.1, bf16[128,256]{1,0:T(8,128)(2,1)} %k_ref.1, bf16[128,256]{1,0:T(8,128)(2,1)} %v_ref.1), custom_call_target="tpu_custom_call" | custom-call | tf_op jit(solution)/shard_map/pallas_call | solution.py:320
  29.2 0.0 copy-start
  29.2 1.8 %copy.10 = bf16[128,1792]{1,0:T(8,128)(2,1)} copy(bf16[128,1792]{1,0:T(8,128)(2,1)} %get-tuple-element.4) | data formatting | bytes 917504
  31.1 0.0 copy-done
  31.1 0.6 %copy.11 = bf16[32,512]{1,0:T(8,128)(2,1)} copy(bf16[32,512]{1,0:T(8,128)(2,1)S(1)} %copy-done) | data formatting | bytes 65536
Async XLA Ops:
  29.2 1.8 %copy-start = (bf16[32,512]{1,0:T(8,128)(2,1)S(1)}, bf16[32,512]{1,0:T(8,128)(2,1)}, u32[]{:S(2)}) copy-start(bf16[32,512]{1,0:T(8,128)(2,1)} %get-tuple-element.5) | copy-start | bytes 98308
